TPU v7x, 32 devices: a whole 2x2x4 slice. The times are simulated.
32 devices in a mesh: band: 4 (over x, core), grid: 8 (over z, y).
Axes of the slice: x: 2, y: 2, z: 4, core: 2. Of those that a mesh axis runs over, the one named last changes fastest.
Arguments:
- orbitals: float32 [8, 128, 128, 128], P('band', 'grid'), may hold values from -6 to 6
- occupation: float32 [8], P('band'), may hold values from 0.25 to 1
- g_list: int32 [131072], P('grid'), may hold values from 0 to 262143, as said below
- positions: float32 [3, 512], replicated, may hold values from 0 to 1
- species: int32 [512], replicated, may hold values from 0 to 3
- widths: float32 [4], replicated, may hold values from 0.3 to 2
Outputs:
- stress: float32 [3, 3], replicated
- atom_terms: float32 [512], replicated
Inputs may be any that keep to these rules, and one draw needn't show every extreme that they name: `g_list`: within each aligned block of 16384 entries the values are distinct and increasing.
All inputs are finite; a program needn't handle non-finite values.
Results may differ from a plain program's by a relative error of at most 0.00013.
Values sent between devices are 32-bit elements; how exact they have to be, the bound alone decides.
No kernel may reach another device: no remote copies, remote signals or barrier semaphores. Data moves between devices by JAX's collectives and lax.ppermute only.
A program may use at most 64 MiB of HBM per device.

v0:
```python
import math
import jax
import jax.numpy as jnp
from jax import lax
from jax.sharding import PartitionSpec as P

HIGHEST = lax.Precision.HIGHEST


def shifted(array, axis, by):
    peers = lax.axis_size(axis)
    return lax.ppermute(array, axis, [(i, (i + by) % peers) for i in range(peers)])


def dft_tables(length):
    indices = jnp.arange(length, dtype=jnp.int32)
    products = indices[:, None] * indices[None, :] % length
    angles = 2.0 * math.pi / length * products.astype(jnp.float32)
    return (jnp.cos(angles), jnp.sin(angles))


def folded_frequency(cell, length):
    folded = jnp.where(cell < length // 2, cell, cell - length)
    return folded.astype(jnp.float32)


def spectrum_sums(
    selected, freq_x, freq_y, freq_z, positions, species, widths, lengths, band_total
):
    two_pi = 2.0 * math.pi
    wave_vector = jnp.stack(
        [two_pi * freq_x / lengths[0], two_pi * freq_y / lengths[1], two_pi * freq_z / lengths[2]]
    )
    wave_square = jnp.sum(wave_vector * wave_vector, axis=0)
    nonzero = (wave_square > 0).astype(jnp.float32)
    denominator = wave_square + 1.0 - nonzero
    weighted = selected * (4.0 * math.pi) * nonzero / denominator
    identity = jnp.eye(3, dtype=jnp.float32)[:, :, None]
    kernel = 2.0 * wave_vector[:, None, :] * wave_vector[None, :, :] / denominator - identity
    stress = jnp.sum(kernel * weighted[None, None, :], axis=2) / band_total
    form_factor = (
        jnp.exp(-0.5 * wave_square[None, :] * (widths * widths)[:, None]) * weighted[None, :]
    )
    kinds = widths.shape[0]
    one_hot = (species[:, None] == jnp.arange(kinds, dtype=jnp.int32)[None, :]).astype(jnp.float32)
    atom_count = species.shape[0]
    fractions = positions.reshape(3, atom_count // 32, 32).transpose(1, 0, 2)
    hot_rows = one_hot.reshape(atom_count // 32, 32, kinds)

    def atom_block(operands):
        fraction, hot_block = operands
        phases = two_pi * (
            fraction[0][:, None] * freq_x[None, :]
            + fraction[1][:, None] * freq_y[None, :]
            + fraction[2][:, None] * freq_z[None, :]
        )
        projected = jnp.dot(jnp.cos(phases), form_factor.T, precision=HIGHEST)
        return jnp.sum(projected * hot_block, axis=1)

    atom_terms = lax.map(atom_block, (fractions, hot_rows)).reshape(atom_count) / band_total
    return (stress, atom_terms)


def per_device(orbitals, occupation, g_list, positions, species, widths):
    block_bands, slab_x, size_y, size_z = orbitals.shape
    grid_count = lax.axis_size("grid")
    band_count = lax.axis_size("band")
    size_x = slab_x * grid_count
    slab_y = size_y // grid_count
    cells = size_x * size_y * size_z
    scale = 1.0 / (float(cells) * float(cells))
    cos_x, sin_x = dft_tables(size_x)
    cos_y, sin_y = dft_tables(size_y)
    cos_z, sin_z = dft_tables(size_z)

    def finish_x(exchanged):
        real_part = exchanged[:, 0]
        imag_part = exchanged[:, 1]
        real_x = jnp.einsum("pxyz,mx->pmyz", real_part, cos_x, precision=HIGHEST) + jnp.einsum(
            "pxyz,mx->pmyz", imag_part, sin_x, precision=HIGHEST
        )
        imag_x = jnp.einsum("pxyz,mx->pmyz", imag_part, cos_x, precision=HIGHEST) - jnp.einsum(
            "pxyz,mx->pmyz", real_part, sin_x, precision=HIGHEST
        )
        return real_x * real_x + imag_x * imag_x

    def add_pairs(accumulated, right_rows, right_occupied, factor):

        def one_band(band_index, running):
            orbital_row = lax.dynamic_index_in_dim(orbitals, band_index, 0, keepdims=False)
            occupied = lax.dynamic_index_in_dim(occupation, band_index, 0, keepdims=False)
            pair_rows = orbital_row[None] * right_rows
            weights = occupied * right_occupied * (factor * scale)
            real_z = jnp.einsum("pxyz,kz->pxyk", pair_rows, cos_z, precision=HIGHEST)
            imag_z = -jnp.einsum("pxyz,kz->pxyk", pair_rows, sin_z, precision=HIGHEST)
            real_y = jnp.einsum("pxyk,my->pxmk", real_z, cos_y, precision=HIGHEST) + jnp.einsum(
                "pxyk,my->pxmk", imag_z, sin_y, precision=HIGHEST
            )
            imag_y = jnp.einsum("pxyk,my->pxmk", imag_z, cos_y, precision=HIGHEST) - jnp.einsum(
                "pxyk,my->pxmk", real_z, sin_y, precision=HIGHEST
            )
            stacked = jnp.stack([real_y, imag_y], axis=1)
            pair_power = finish_x(
                lax.all_to_all(stacked, "grid", split_axis=3, concat_axis=2, tiled=True)
            )
            return running + jnp.einsum("p,pxyz->xyz", weights, pair_power, precision=HIGHEST)

        return lax.fori_loop(0, block_bands, one_band, accumulated)

    empty = jnp.zeros((size_x, slab_y, size_z), jnp.float32)
    spectrum = add_pairs(empty, orbitals, occupation, 1.0)
    for distance in range(1, band_count // 2 + 1):
        neighbour = shifted((orbitals, occupation), "band", distance)
        factor = 2.0 if 2 * distance < band_count else 1.0
        spectrum = add_pairs(spectrum, neighbour[0], neighbour[1], factor)
    flat_spectrum = spectrum.reshape(-1)
    selected = jnp.take(flat_spectrum, g_list)
    cell_x = g_list // (slab_y * size_z)
    cell_y = lax.axis_index("grid") * slab_y + g_list // size_z % slab_y
    cell_z = g_list % size_z
    stress, atom_terms = spectrum_sums(
        selected,
        folded_frequency(cell_x, size_x),
        folded_frequency(cell_y, size_y),
        folded_frequency(cell_z, size_z),
        positions,
        species,
        widths,
        (size_x, size_y, size_z),
        block_bands * band_count,
    )
    stress, atom_terms = lax.psum((stress, atom_terms), ("band", "grid"))
    return (stress, atom_terms)


def solution(mesh):
    return jax.shard_map(
        per_device,
        mesh=mesh,
        in_specs=(P("band", "grid", None, None), P("band"), P("grid"), P(), P(), P()),
        out_specs=(P(), P()),
        check_vma=False,
    )
```

profile of v0, /device:TPU:12, one launch (start us, length us, event | category | flops | bytes accessed | tf_op | source)
XLA Modules:
  0.0 1331.4 jit_solution(5733320906474539223)
XLA Ops:
  13.5 339.4 %while.62 = (s32[]{:T(128)}, f32[128,16,128]{2,1,0:T(8,128)S(1)}, f32[2]{0:T(128)}, f32[2,16,128,128]{3,2,1,0:T(8,128)}, s32[]{:T(128)}, /*index=5*/s32[]{:T(128)}) while((s32[]{:T(128)}, f32[128,16,128]{2,1,0:T(8,128)S(1)}, f32[2]{0:T(128)}, f32[2,16,128,128]{3,2,1,0:T(8,128)}, s32[]{:T(128)}, ...), condition=%wide.region_2.3_spmd.clone.clone, body=%wide.region_1.2_spmd.clone.clone.sunk | while | flops 8068988928 | bytes 146800944 | solution.py:108
  33.9 5.5 copy.157
  39.4 6.4 all-to-all-start.2
  46.4 89.6 %all-to-all-done.2 = f32[2,2,16,128,128]{4,2,0,1,3:T(8,128)} async-done(((f32[2,2,16,128,128]{4,2,0,1,3:T(8,128)}), f32[2,2,16,128,128]{4,2,0,1,3:T(8,128)}, u32[]{:S(2)}, u32[]{:S(2)}) %all-to-all-start.2) | async-done | bytes 4194336 | tf_op jit(solution)/shard_map/while/body/eval_jaxpr/all_to_all | solution.py:104
  135.9 4.6 copy.158
  162.9 8.2 fusion.552
  192.0 5.5 copy.157
  197.4 8.0 all-to-all-start.2
  206.0 88.7 %all-to-all-done.2 = f32[2,2,16,128,128]{4,2,0,1,3:T(8,128)} async-done(((f32[2,2,16,128,128]{4,2,0,1,3:T(8,128)}), f32[2,2,16,128,128]{4,2,0,1,3:T(8,128)}, u32[]{:S(2)}, u32[]{:S(2)}) %all-to-all-start.2) | async-done | bytes 4194336 | tf_op jit(solution)/shard_map/while/body/eval_jaxpr/all_to_all | solution.py:104
  321.8 8.2 fusion.552
  352.9 323.8 %while.60 = (s32[]{:T(128)}, f32[128,16,128]{2,1,0:T(8,128)S(1)}, f32[2]{0:T(128)}, f32[2]{0:T(128)}, f32[2,16,128,128]{3,2,1,0:T(8,128)}, /*index=5*/f32[2,16,128,128]{3,2,1,0:T(8,128)}, s32[]{:T(128)}) while((s32[]{:T(128)}, f32[128,16,128]{2,1,0:T(8,128)S(1)}, f32[2]{0:T(128)}, f32[2]{0:T(128)}, ...), condition=%wide.region_4.5_spmd.clone.clone, body=%wide.region_3.4_spmd.clone.clone.sunk | while | flops 8068726784 | bytes 138412304 | solution.py:108
  375.9 5.5 copy.147
  381.4 8.0 all-to-all-start
  390.0 88.6 %all-to-all-done = f32[2,2,16,128,128]{4,2,0,1,3:T(8,128)} async-done(((f32[2,2,16,128,128]{4,2,0,1,3:T(8,128)}), f32[2,2,16,128,128]{4,2,0,1,3:T(8,128)}, u32[]{:S(2)}, u32[]{:S(2)}) %all-to-all-start) | async-done | bytes 4194336 | tf_op jit(solution)/shard_map/while/body/eval_jaxpr/all_to_all | solution.py:104
  505.7 8.9 fusion.492
  537.9 5.5 copy.147
  543.4 8.0 all-to-all-start
  551.9 88.6 %all-to-all-done = f32[2,2,16,128,128]{4,2,0,1,3:T(8,128)} async-done(((f32[2,2,16,128,128]{4,2,0,1,3:T(8,128)}), f32[2,2,16,128,128]{4,2,0,1,3:T(8,128)}, u32[]{:S(2)}, u32[]{:S(2)}) %all-to-all-start) | async-done | bytes 4194336 | tf_op jit(solution)/shard_map/while/body/eval_jaxpr/all_to_all | solution.py:104
  640.6 4.6 copy.148
  667.6 8.9 fusion.492
  676.8 354.2 %while.61 = (s32[]{:T(128)}, f32[128,16,128]{2,1,0:T(8,128)S(1)}, f32[2]{0:T(128)}, f32[2]{0:T(128)}, f32[2,16,128,128]{3,2,1,0:T(8,128)}, /*index=5*/f32[2,16,128,128]{3,2,1,0:T(8,128)}, s32[]{:T(128)}) while((s32[]{:T(128)}, f32[128,16,128]{2,1,0:T(8,128)S(1)}, f32[2]{0:T(128)}, f32[2]{0:T(128)}, ...), condition=%wide.region_6.7_spmd.clone.clone, body=%wide.region_5.6_spmd.clone.clone.sunk | while | flops 8068726784 | bytes 138412304 | solution.py:108
  722.3 5.5 copy.152
  727.8 8.0 all-to-all-start.1
  736.4 88.7 %all-to-all-done.1 = f32[2,2,16,128,128]{4,2,0,1,3:T(8,128)} async-done(((f32[2,2,16,128,128]{4,2,0,1,3:T(8,128)}), f32[2,2,16,128,128]{4,2,0,1,3:T(8,128)}, u32[]{:S(2)}, u32[]{:S(2)}) %all-to-all-start.1) | async-done | bytes 4194336 | tf_op jit(solution)/shard_map/while/body/eval_jaxpr/all_to_all | solution.py:104
  852.1 8.9 fusion.522
  884.3 5.5 copy.152
  889.7 8.0 all-to-all-start.1
  898.3 88.7 %all-to-all-done.1 = f32[2,2,16,128,128]{4,2,0,1,3:T(8,128)} async-done(((f32[2,2,16,128,128]{4,2,0,1,3:T(8,128)}), f32[2,2,16,128,128]{4,2,0,1,3:T(8,128)}, u32[]{:S(2)}, u32[]{:S(2)}) %all-to-all-start.1) | async-done | bytes 4194336 | tf_op jit(solution)/shard_map/while/body/eval_jaxpr/all_to_all | solution.py:104
  1014.0 8.9 fusion.522
  1031.1 90.5 %gather_fusion = f32[16384]{0:T(1024)S(1)} fusion(f32[262144]{0:T(1024)S(1)} %bitcast.377, s32[16384]{0:T(1024)S(1)} %copy-done.11), kind=kCustom, calls=%fused_computation | custom fusion | bytes 196608 | tf_op jit(solution)/shard_map/jit(_take)/gather | solution.py:117
  1122.3 166.4 %while.59 = (s32[]{:T(128)}, f32[16,32]{1,0:T(8,128)S(1)}, f32[16,3,32]{2,0,1:T(8,128)}, f32[16384]{0:T(1024)S(1)}, f32[16384]{0:T(1024)S(1)}, /*index=5*/f32[16...) while((s32[]{:T(128)}, f32[16,32]{1,0:T(8,128)S(1)}, ...), condition=%wide.region_11.12_spmd.clone, body=%wide.region_9.11_spmd.clone.sunk | while | flops 28442852 | bytes 329921 | solution.py:60
  1123.0 9.6 fusion.462
  1133.4 9.6 fusion.462
  1143.8 9.6 fusion.462
  1154.2 9.6 fusion.462
  1164.6 9.6 fusion.462
  1175.0 9.6 fusion.462
  1185.4 9.6 fusion.462
  1195.8 9.7 fusion.462
  1206.2 9.6 fusion.462
  1216.6 9.7 fusion.462
  1227.1 9.6 fusion.462
  1237.5 9.7 fusion.462
  1247.9 9.6 fusion.462
  1258.3 9.6 fusion.462
  1268.7 9.6 fusion.462
  1279.1 9.6 fusion.462
  1288.8 42.1 %all-reduce = (f32[3,3]{1,0:T(4,128)}, f32[512]{0:T(512)}) all-reduce(f32[3,3]{1,0:T(4,128)S(1)} %broadcast_multiply_fusion.6, f32[512]{0:T(512)S(1)} %div.77), channel_id=1, replica_groups=mesh['band'=4,'grid'=8] {'band','grid'}, use_global_device_ids=true, to_apply=%region_8.9 | all-reduce | flops 521 | bytes 4168 | tf_op jit(solution)/shard_map/psum | solution.py:132
  (229 shorter events, 315.7 us)
Async XLA Ops:
  0.6 352.2 %collective-permute-start.1 = (f32[2,16,128,128]{3,2,1,0:T(8,128)}, f32[2,16,128,128]{3,2,1,0:T(8,128)}, u32[]{:S(2)}, u32[]{:S(2)}) collective-permute-start(f32[2,16,128,128]{3,2,1,0:T(8,128)} %param.14), channel_id=1, source_target_pairs={{0,8},{8,16},{16,24},{24,0},{1,9},{9,17},{17,25},{25,1},{2,10},{10... | collective-permute-start | bytes 6291464 | tf_op jit(solution)/shard_map/ppermute | solution.py:12
  0.7 676.0 %collective-permute-start.3 = (f32[2,16,128,128]{3,2,1,0:T(8,128)}, f32[2,16,128,128]{3,2,1,0:T(8,128)}, u32[]{:S(2)}, u32[]{:S(2)}) collective-permute-start(f32[2,16,128,128]{3,2,1,0:T(8,128)} %param.14), channel_id=1, source_target_pairs={{0,16},{8,24},{16,0},{24,8},{1,17},{9,25},{17,1},{25,9},{2,18},{10... | collective-permute-start | bytes 6291464 | tf_op jit(solution)/shard_map/ppermute | solution.py:12
  2.3 350.6 %collective-permute-start = (f32[2]{0:T(128)}, f32[2]{0:T(128)}, u32[]{:S(2)}, u32[]{:S(2)}) collective-permute-start(f32[2]{0:T(128)} %param.15), channel_id=1, source_target_pairs={{0,8},{8,16},{16,24},{24,0},{1,9},{9,17},{17,25},{25,1},{2,10},{10... | collective-permute-start | bytes 32 | tf_op jit(solution)/shard_map/ppermute | solution.py:12
  2.5 350.3 %collective-permute-start.2 = (f32[2]{0:T(128)}, f32[2]{0:T(128)}, u32[]{:S(2)}, u32[]{:S(2)}) collective-permute-start(f32[2]{0:T(128)} %param.15), channel_id=1, source_target_pairs={{0,16},{8,24},{16,0},{24,8},{1,17},{9,25},{17,1},{25,9},{2,18},{10... | collective-permute-start | bytes 32 | tf_op jit(solution)/shard_map/ppermute | solution.py:12
  13.5 1.9 copy-start
  39.4 6.4 copy-start.17
  39.4 96.5 %all-to-all-start.2 = ((f32[2,2,16,128,128]{4,2,0,1,3:T(8,128)}), f32[2,2,16,128,128]{4,2,0,1,3:T(8,128)}, u32[]{:S(2)}, u32[]{:S(2)}) async-start(f32[2,2,16,128,128]{4,2,0,1,3:T(8,128)} %copy.157), calls=%async_computation.2 | async-start | bytes 8388608 | tf_op jit(solution)/shard_map/while/body/eval_jaxpr/all_to_all | solution.py:104
  153.5 2.1 copy-start.1
  153.5 2.2 copy-start.2
  171.5 1.9 copy-start
  197.4 8.0 copy-start.17
  197.4 97.3 %all-to-all-start.2 = ((f32[2,2,16,128,128]{4,2,0,1,3:T(8,128)}), f32[2,2,16,128,128]{4,2,0,1,3:T(8,128)}, u32[]{:S(2)}, u32[]{:S(2)}) async-start(f32[2,2,16,128,128]{4,2,0,1,3:T(8,128)} %copy.157), calls=%async_computation.2 | async-start | bytes 8388608 | tf_op jit(solution)/shard_map/while/body/eval_jaxpr/all_to_all | solution.py:104
  312.3 2.1 copy-start.1
  312.3 2.2 copy-start.2
  381.4 8.0 copy-start.18
  381.4 97.2 %all-to-all-start = ((f32[2,2,16,128,128]{4,2,0,1,3:T(8,128)}), f32[2,2,16,128,128]{4,2,0,1,3:T(8,128)}, u32[]{:S(2)}, u32[]{:S(2)}) async-start(f32[2,2,16,128,128]{4,2,0,1,3:T(8,128)} %copy.147), calls=%async_computation | async-start | bytes 8388608 | tf_op jit(solution)/shard_map/while/body/eval_jaxpr/all_to_all | solution.py:104
  496.2 2.1 copy-start.3
  496.2 2.2 copy-start.4
  543.4 8.0 copy-start.18
  543.4 97.2 %all-to-all-start = ((f32[2,2,16,128,128]{4,2,0,1,3:T(8,128)}), f32[2,2,16,128,128]{4,2,0,1,3:T(8,128)}, u32[]{:S(2)}, u32[]{:S(2)}) async-start(f32[2,2,16,128,128]{4,2,0,1,3:T(8,128)} %copy.147), calls=%async_computation | async-start | bytes 8388608 | tf_op jit(solution)/shard_map/while/body/eval_jaxpr/all_to_all | solution.py:104
  658.1 2.1 copy-start.3
  658.1 2.2 copy-start.4
  676.7 354.3 %copy-start.11 = (s32[16384]{0:T(1024)S(1)}, s32[16384]{0:T(1024)}, u32[]{:S(2)}) copy-start(s32[16384]{0:T(1024)} %fusion.346) | copy-start | bytes 196612
  727.8 8.0 copy-start.19
  727.8 97.2 %all-to-all-start.1 = ((f32[2,2,16,128,128]{4,2,0,1,3:T(8,128)}), f32[2,2,16,128,128]{4,2,0,1,3:T(8,128)}, u32[]{:S(2)}, u32[]{:S(2)}) async-start(f32[2,2,16,128,128]{4,2,0,1,3:T(8,128)} %copy.152), calls=%async_computation.1 | async-start | bytes 8388608 | tf_op jit(solution)/shard_map/while/body/eval_jaxpr/all_to_all | solution.py:104
  842.6 2.1 copy-start.5
  842.6 2.2 copy-start.6
  889.7 8.0 copy-start.19
  889.7 97.2 %all-to-all-start.1 = ((f32[2,2,16,128,128]{4,2,0,1,3:T(8,128)}), f32[2,2,16,128,128]{4,2,0,1,3:T(8,128)}, u32[]{:S(2)}, u32[]{:S(2)}) async-start(f32[2,2,16,128,128]{4,2,0,1,3:T(8,128)} %copy.152), calls=%async_computation.1 | async-start | bytes 8388608 | tf_op jit(solution)/shard_map/while/body/eval_jaxpr/all_to_all | solution.py:104
  1004.5 2.1 copy-start.5
  1004.5 2.2 copy-start.6
  1031.0 90.7 %copy-start.9 = (s32[16384]{0:T(1024)S(1)}, s32[16384]{0:T(1024)}, u32[]{:S(2)}) copy-start(s32[16384]{0:T(1024)} %param.16) | copy-start | bytes 196612
  1031.0 90.6 %copy-start.10 = (f32[16384]{0:T(1024)S(1)}, f32[16384]{0:T(1024)}, u32[]{:S(2)}) copy-start(f32[16384]{0:T(1024)} %get-tuple-element.865) | copy-start | bytes 196612
  1031.0 90.7 %copy-start.7 = (f32[3,16384]{1,0:T(4,128)S(1)}, f32[3,16384]{1,0:T(4,128)}, u32[]{:S(2)}) copy-start(f32[3,16384]{1,0:T(4,128)} %get-tuple-element.864) | copy-start | bytes 589828
  1031.0 90.7 %copy-start.8 = (f32[3,16384]{1,0:T(4,128)S(1)}, f32[3,16384]{1,0:T(4,128)}, u32[]{:S(2)}) copy-start(f32[3,16384]{1,0:T(4,128)} %get-tuple-element.866) | copy-start | bytes 589828
  1031.1 90.7 %copy-start.15 = (f32[3,3]{1,0:T(4,128)S(1)}, f32[3,3]{1,0:T(4,128)}, u32[]{:S(2)}) copy-start(f32[3,3]{1,0:T(4,128)} %fusion.349) | copy-start | bytes 112
  1031.1 91.2 %copy-start.12 = (f32[16384]{0:T(1024)S(1)}, f32[16384]{0:T(1024)}, u32[]{:S(2)}) copy-start(f32[16384]{0:T(1024)} %get-tuple-element.1115) | copy-start | bytes 196612
  1031.1 91.2 %copy-start.13 = (f32[16384]{0:T(1024)S(1)}, f32[16384]{0:T(1024)}, u32[]{:S(2)}) copy-start(f32[16384]{0:T(1024)} %get-tuple-element.1117) | copy-start | bytes 196612
  1031.1 91.2 %copy-start.14 = (f32[16384]{0:T(1024)S(1)}, f32[16384]{0:T(1024)}, u32[]{:S(2)}) copy-start(f32[16384]{0:T(1024)} %get-tuple-element.1116) | copy-start | bytes 196612
  1031.1 91.2 %copy-start.16 = (f32[16,32]{1,0:T(8,128)S(1)}, f32[16,32]{1,0:T(8,128)}, u32[]{:S(2)}) copy-start(f32[16,32]{1,0:T(8,128)} %custom-call.3) | copy-start | bytes 6148
  1031.1 91.2 %copy-start.20 = (f32[4]{0:T(128)S(1)}, f32[4]{0:T(128)}, u32[]{:S(2)}) copy-start(f32[4]{0:T(128)} %mul.627) | copy-start | bytes 52
where the time goes:
time: 1360 us; the launch traced here: 1330 us
  waiting for transfers between devices  533 us (39%)
  matrix products  391 us (29%)
  local copies, waits for them, and re-layouts  237 us (17%)
  loops' own time  54.2 us (4%)
  starting transfers between devices  49.7 us (4%)
  blocking collectives  42.1 us (3%)
  other arithmetic  23.1 us (2%)
    all_to_all x6, waiting for transfers between devices, one_band(): lax.all_to_all(stacked, 'grid', split_axis=3, concat_axis=2, tiled=True)  533 us
    dot_general x16, matrix products, atom_block(): projected = jnp.dot(jnp.cos(phases), form_factor.T, precision=HIGHEST)  154 us
    gather x1, local copies, waits for them, and re-layouts, per_device(): selected = jnp.take(flat_spectrum, g_list)  90.5 us
    another operation x3, loops' own time, add_pairs(): return lax.fori_loop(0, block_bands, one_band, accumulated)  53.9 us
    dot_general x6, matrix products, one_band(): jnp.einsum('p,pxyz->xyz', weights, pair_power, precision=HIGHEST)  52 us
    all_to_all x6, starting transfers between devices, one_band(): lax.all_to_all(stacked, 'grid', split_axis=3, concat_axis=2, tiled=True)  46.3 us
    psum x1, blocking collectives, per_device(): stress, atom_terms = lax.psum((stress, atom_terms), ('band', 'grid'))  42.1 us
    another operation x6, local copies, waits for them, and re-layouts, one_band(): stacked = jnp.stack([real_y, imag_y], axis=1)  32.8 us
  transfers between devices with their start and end apart: 10, of which 6 were waited for; matrix products, arithmetic and copies ran while one was open for 20% of the time, Pallas kernels for 0%

commit v1 on v0

--- a/solution.py
+++ b/solution.py
@@ -5,6 +5,12 @@
 from jax.sharding import PartitionSpec as P
 
 HIGHEST = lax.Precision.HIGHEST
+
+
+def exchange_blocks(x, axis, split, join):
+    pieces = jnp.split(x, lax.axis_size(axis), axis=split)
+    received = lax.all_to_all(jnp.stack(pieces), axis, 0, 0)
+    return jnp.concatenate(received, axis=join)
 
 
 def shifted(array, axis, by):
@@ -100,9 +106,7 @@
                 "pxyk,my->pxmk", real_z, sin_y, precision=HIGHEST
             )
             stacked = jnp.stack([real_y, imag_y], axis=1)
-            pair_power = finish_x(
-                lax.all_to_all(stacked, "grid", split_axis=3, concat_axis=2, tiled=True)
-            )
+            pair_power = finish_x(exchange_blocks(stacked, "grid", 3, 2))
             return running + jnp.einsum("p,pxyz->xyz", weights, pair_power, precision=HIGHEST)
 
         return lax.fori_loop(0, block_bands, one_band, accumulated)

time: 1360 us -> 1310 us (0.963)
  local copies, waits for them, and re-layouts: 237 us -> 191 us
  other arithmetic: 23.1 us -> 50.4 us
  matrix products: 391 us -> 375 us
    while x0 -> x42, other arithmetic: none -> 35.7 us
    another operation x6 -> x0, local copies, waits for them, and re-layouts: 32.8 us -> none  [one_band(): stacked = jnp.stack([real_y, imag_y], axis=1)]
    all_to_all x6 -> x0, local copies, waits for them, and re-layouts: 27.7 us -> none  [one_band(): lax.all_to_all(stacked, 'grid', split_axis=3, concat_axis=2, tiled=True)]
    reshape x0 -> x6, local copies, waits for them, and re-layouts: none -> 15.3 us  [exchange_blocks(): return jnp.concatenate(received, axis=join)]
  transfers between devices with their start and end apart: 10 -> 10, of which waited for: 6 -> 6; matrix products, arithmetic and copies ran while one was open for 20% -> 19% of each run, Pallas kernels for 0% -> 0%
where the time goes in v1:
time: 1310 us; the launch traced here: 1290 us
  waiting for transfers between devices  533 us (41%)
  matrix products  375 us (29%)
  local copies, waits for them, and re-layouts  191 us (15%)
  other arithmetic  50.4 us (4%)
  starting transfers between devices  49.7 us (4%)
  loops' own time  47.7 us (4%)
  blocking collectives  42.1 us (3%)
    all_to_all x6, waiting for transfers between devices, exchange_blocks(): received = lax.all_to_all(jnp.stack(pieces), axis, 0, 0)  533 us
    dot_general x16, matrix products, atom_block(): projected = jnp.dot(jnp.cos(phases), form_factor.T, precision=HIGHEST)  154 us
    gather x1, local copies, waits for them, and re-layouts, per_device(): selected = jnp.take(flat_spectrum, g_list)  90.5 us
    dot_general x6, matrix products, one_band(): jnp.einsum('p,pxyz->xyz', weights, pair_power, precision=HIGHEST)  52 us
    another operation x3, loops' own time, add_pairs(): return lax.fori_loop(0, block_bands, one_band, accumulated)  47.3 us
    all_to_all x6, starting transfers between devices, exchange_blocks(): received = lax.all_to_all(jnp.stack(pieces), axis, 0, 0)  46.3 us
    psum x1, blocking collectives, per_device(): stress, atom_terms = lax.psum((stress, atom_terms), ('band', 'grid'))  42.1 us
    while x42, other arithmetic  35.7 us
  transfers between devices with their start and end apart: 10, of which 6 were waited for; matrix products, arithmetic and copies ran while one was open for 19% of the time, Pallas kernels for 0%

profile of v1, /device:TPU:12, one launch (start us, length us, event | category | flops | bytes accessed | tf_op | source)
XLA Modules:
  0.0 1290.0 jit_solution(17536911958422384852)
XLA Ops:
  13.5 324.5 %while.62 = (s32[]{:T(128)}, f32[128,16,128]{2,1,0:T(8,128)S(1)}, f32[2]{0:T(128)}, f32[2,16,128,128]{3,2,1,0:T(8,128)}, s32[]{:T(128)}, /*index=5*/s32[]{:T(128)}) while((s32[]{:T(128)}, f32[128,16,128]{2,1,0:T(8,128)S(1)}, f32[2]{0:T(128)}, f32[2,16,128,128]{3,2,1,0:T(8,128)}, s32[]{:T(128)}, ...), condition=%wide.region_2.3_spmd.clone.clone, body=%wide.region_1.2_spmd.clone.clone.sunk | while | flops 8068988928 | bytes 167772464 | solution.py:112
  35.7 6.4 all-to-all-start.2
  42.6 89.6 %all-to-all-done.2 = f32[8,2,2,16,16,128]{5,4,3,1,2,0:T(8,128)} async-done(((f32[8,2,2,16,16,128]{5,4,3,1,2,0:T(8,128)}), f32[8,2,2,16,16,128]{5,4,3,1,2,0:T(8,128)}, u32[]{:S(2)}, u32[]{:S(2)}) %all-to-all-start.2) | async-done | bytes 4194336 | tf_op jit(solution)/shard_map/while/body/eval_jaxpr/all_to_all | solution.py:12
  157.1 8.2 fusion.669
  187.9 8.0 all-to-all-start.2
  196.5 88.7 %all-to-all-done.2 = f32[8,2,2,16,16,128]{5,4,3,1,2,0:T(8,128)} async-done(((f32[8,2,2,16,16,128]{5,4,3,1,2,0:T(8,128)}), f32[8,2,2,16,16,128]{5,4,3,1,2,0:T(8,128)}, u32[]{:S(2)}, u32[]{:S(2)}) %all-to-all-start.2) | async-done | bytes 4194336 | tf_op jit(solution)/shard_map/while/body/eval_jaxpr/all_to_all | solution.py:12
  310.2 8.3 fusion.669
  338.0 312.3 %while.60 = (s32[]{:T(128)}, f32[128,16,128]{2,1,0:T(8,128)S(1)}, f32[2]{0:T(128)}, f32[2]{0:T(128)}, f32[2,16,128,128]{3,2,1,0:T(8,128)}, /*index=5*/f32[2,16,128,128]{3,2,1,0:T(8,128)}, s32[]{:T(128)}) while((s32[]{:T(128)}, f32[128,16,128]{2,1,0:T(8,128)S(1)}, f32[2]{0:T(128)}, f32[2]{0:T(128)}, ...), condition=%wide.region_4.5_spmd.clone.clone, body=%wide.region_3.4_spmd.clone.clone.sunk | while | flops 8068726784 | bytes 159383824 | solution.py:112
  339.3 3.7 fusion.577
  343.1 3.7 fusion.579
  362.8 8.0 all-to-all-start
  371.4 88.6 %all-to-all-done = f32[8,2,2,16,16,128]{5,4,3,1,2,0:T(8,128)} async-done(((f32[8,2,2,16,16,128]{5,4,3,1,2,0:T(8,128)}), f32[8,2,2,16,16,128]{5,4,3,1,2,0:T(8,128)}, u32[]{:S(2)}, u32[]{:S(2)}) %all-to-all-start) | async-done | bytes 4194336 | tf_op jit(solution)/shard_map/while/body/eval_jaxpr/all_to_all | solution.py:12
  485.0 8.9 fusion.593
  495.5 3.7 fusion.577
  499.2 3.7 fusion.579
  519.0 8.0 all-to-all-start
  527.6 88.6 %all-to-all-done = f32[8,2,2,16,16,128]{5,4,3,1,2,0:T(8,128)} async-done(((f32[8,2,2,16,16,128]{5,4,3,1,2,0:T(8,128)}), f32[8,2,2,16,16,128]{5,4,3,1,2,0:T(8,128)}, u32[]{:S(2)}, u32[]{:S(2)}) %all-to-all-start) | async-done | bytes 4194336 | tf_op jit(solution)/shard_map/while/body/eval_jaxpr/all_to_all | solution.py:12
  641.2 8.9 fusion.593
  650.3 339.4 %while.61 = (s32[]{:T(128)}, f32[128,16,128]{2,1,0:T(8,128)S(1)}, f32[2]{0:T(128)}, f32[2]{0:T(128)}, f32[2,16,128,128]{3,2,1,0:T(8,128)}, /*index=5*/f32[2,16,128,128]{3,2,1,0:T(8,128)}, s32[]{:T(128)}) while((s32[]{:T(128)}, f32[128,16,128]{2,1,0:T(8,128)S(1)}, f32[2]{0:T(128)}, f32[2]{0:T(128)}, ...), condition=%wide.region_6.7_spmd.clone.clone, body=%wide.region_5.6_spmd.clone.clone.sunk | while | flops 8068726784 | bytes 159383824 | solution.py:112
  670.8 3.7 fusion.615
  674.6 3.7 fusion.617
  694.4 8.0 all-to-all-start.1
  702.9 88.7 %all-to-all-done.1 = f32[8,2,2,16,16,128]{5,4,3,1,2,0:T(8,128)} async-done(((f32[8,2,2,16,16,128]{5,4,3,1,2,0:T(8,128)}), f32[8,2,2,16,16,128]{5,4,3,1,2,0:T(8,128)}, u32[]{:S(2)}, u32[]{:S(2)}) %all-to-all-start.1) | async-done | bytes 4194336 | tf_op jit(solution)/shard_map/while/body/eval_jaxpr/all_to_all | solution.py:12
  816.5 8.9 fusion.631
  827.0 3.7 fusion.615
  830.7 3.7 fusion.617
  850.5 8.0 all-to-all-start.1
  859.1 88.7 %all-to-all-done.1 = f32[8,2,2,16,16,128]{5,4,3,1,2,0:T(8,128)} async-done(((f32[8,2,2,16,16,128]{5,4,3,1,2,0:T(8,128)}), f32[8,2,2,16,16,128]{5,4,3,1,2,0:T(8,128)}, u32[]{:S(2)}, u32[]{:S(2)}) %all-to-all-start.1) | async-done | bytes 4194336 | tf_op jit(solution)/shard_map/while/body/eval_jaxpr/all_to_all | solution.py:12
  972.7 8.9 fusion.631
  989.8 90.5 %gather_fusion = f32[16384]{0:T(1024)S(1)} fusion(f32[262144]{0:T(1024)S(1)} %bitcast.515, s32[16384]{0:T(1024)S(1)} %copy-done.11), kind=kCustom, calls=%fused_computation | custom fusion | bytes 196608 | tf_op jit(solution)/shard_map/jit(_take)/gather | solution.py:121
  1081.0 166.4 %while.59 = (s32[]{:T(128)}, f32[16,32]{1,0:T(8,128)S(1)}, f32[16,3,32]{2,0,1:T(8,128)}, f32[16384]{0:T(1024)S(1)}, f32[16384]{0:T(1024)S(1)}, /*index=5*/f32[16...) while((s32[]{:T(128)}, f32[16,32]{1,0:T(8,128)S(1)}, ...), condition=%wide.region_11.12_spmd.clone, body=%wide.region_9.11_spmd.clone.sunk | while | flops 28442852 | bytes 329921 | solution.py:66
  1081.7 9.6 fusion.555
  1092.1 9.6 fusion.555
  1102.5 9.6 fusion.555
  1112.9 9.6 fusion.555
  1123.3 9.6 fusion.555
  1133.7 9.6 fusion.555
  1144.1 9.6 fusion.555
  1154.5 9.7 fusion.555
  1164.9 9.6 fusion.555
  1175.3 9.7 fusion.555
  1185.7 9.6 fusion.555
  1196.1 9.7 fusion.555
  1206.6 9.6 fusion.555
  1217.0 9.6 fusion.555
  1227.3 9.6 fusion.555
  1237.7 9.6 fusion.555
  1247.5 42.1 %all-reduce = (f32[3,3]{1,0:T(4,128)}, f32[512]{0:T(512)}) all-reduce(f32[3,3]{1,0:T(4,128)S(1)} %broadcast_multiply_fusion.6, f32[512]{0:T(512)S(1)} %div.77), channel_id=1, replica_groups=mesh['band'=4,'grid'=8] {'band','grid'}, use_global_device_ids=true, to_apply=%region_8.9 | all-reduce | flops 521 | bytes 4168 | tf_op jit(solution)/shard_map/psum | solution.py:136
  (265 shorter events, 293.1 us)
Async XLA Ops:
  0.6 337.4 %collective-permute-start.1 = (f32[2,16,128,128]{3,2,1,0:T(8,128)}, f32[2,16,128,128]{3,2,1,0:T(8,128)}, u32[]{:S(2)}, u32[]{:S(2)}) collective-permute-start(f32[2,16,128,128]{3,2,1,0:T(8,128)} %param.14), channel_id=1, source_target_pairs={{0,8},{8,16},{16,24},{24,0},{1,9},{9,17},{17,25},{25,1},{2,10},{10... | collective-permute-start | bytes 6291464 | tf_op jit(solution)/shard_map/ppermute | solution.py:18
  0.7 649.6 %collective-permute-start.3 = (f32[2,16,128,128]{3,2,1,0:T(8,128)}, f32[2,16,128,128]{3,2,1,0:T(8,128)}, u32[]{:S(2)}, u32[]{:S(2)}) collective-permute-start(f32[2,16,128,128]{3,2,1,0:T(8,128)} %param.14), channel_id=1, source_target_pairs={{0,16},{8,24},{16,0},{24,8},{1,17},{9,25},{17,1},{25,9},{2,18},{10... | collective-permute-start | bytes 6291464 | tf_op jit(solution)/shard_map/ppermute | solution.py:18
  2.3 335.7 %collective-permute-start = (f32[2]{0:T(128)}, f32[2]{0:T(128)}, u32[]{:S(2)}, u32[]{:S(2)}) collective-permute-start(f32[2]{0:T(128)} %param.15), channel_id=1, source_target_pairs={{0,8},{8,16},{16,24},{24,0},{1,9},{9,17},{17,25},{25,1},{2,10},{10... | collective-permute-start | bytes 32 | tf_op jit(solution)/shard_map/ppermute | solution.py:18
  2.5 335.4 %collective-permute-start.2 = (f32[2]{0:T(128)}, f32[2]{0:T(128)}, u32[]{:S(2)}, u32[]{:S(2)}) collective-permute-start(f32[2]{0:T(128)} %param.15), channel_id=1, source_target_pairs={{0,16},{8,24},{16,0},{24,8},{1,17},{9,25},{17,1},{25,9},{2,18},{10... | collective-permute-start | bytes 32 | tf_op jit(solution)/shard_map/ppermute | solution.py:18
  13.5 1.9 copy-start
  35.7 6.4 copy-start.17
  35.7 96.5 %all-to-all-start.2 = ((f32[8,2,2,16,16,128]{5,4,3,1,2,0:T(8,128)}), f32[8,2,2,16,16,128]{5,4,3,1,2,0:T(8,128)}, u32[]{:S(2)}, u32[]{:S(2)}) async-start(f32[8,2,2,16,16,128]{5,4,3,1,2,0:T(8,128)} %fusion.664), calls=%async_computation.2 | async-start | bytes 8388608 | tf_op jit(solution)/shard_map/while/body/eval_jaxpr/all_to_all | solution.py:12
  147.7 2.1 copy-start.1
  147.7 2.2 copy-start.2
  165.7 1.9 copy-start
  187.9 8.0 copy-start.17
  187.9 97.3 %all-to-all-start.2 = ((f32[8,2,2,16,16,128]{5,4,3,1,2,0:T(8,128)}), f32[8,2,2,16,16,128]{5,4,3,1,2,0:T(8,128)}, u32[]{:S(2)}, u32[]{:S(2)}) async-start(f32[8,2,2,16,16,128]{5,4,3,1,2,0:T(8,128)} %fusion.664), calls=%async_computation.2 | async-start | bytes 8388608 | tf_op jit(solution)/shard_map/while/body/eval_jaxpr/all_to_all | solution.py:12
  300.7 2.1 copy-start.1
  300.7 2.2 copy-start.2
  362.8 8.0 copy-start.18
  362.8 97.2 %all-to-all-start = ((f32[8,2,2,16,16,128]{5,4,3,1,2,0:T(8,128)}), f32[8,2,2,16,16,128]{5,4,3,1,2,0:T(8,128)}, u32[]{:S(2)}, u32[]{:S(2)}) async-start(f32[8,2,2,16,16,128]{5,4,3,1,2,0:T(8,128)} %fusion.588), calls=%async_computation | async-start | bytes 8388608 | tf_op jit(solution)/shard_map/while/body/eval_jaxpr/all_to_all | solution.py:12
  475.6 2.1 copy-start.3
  475.6 2.2 copy-start.4
  519.0 8.0 copy-start.18
  519.0 97.2 %all-to-all-start = ((f32[8,2,2,16,16,128]{5,4,3,1,2,0:T(8,128)}), f32[8,2,2,16,16,128]{5,4,3,1,2,0:T(8,128)}, u32[]{:S(2)}, u32[]{:S(2)}) async-start(f32[8,2,2,16,16,128]{5,4,3,1,2,0:T(8,128)} %fusion.588), calls=%async_computation | async-start | bytes 8388608 | tf_op jit(solution)/shard_map/while/body/eval_jaxpr/all_to_all | solution.py:12
  631.7 2.1 copy-start.3
  631.7 2.2 copy-start.4
  650.3 339.4 %copy-start.11 = (s32[16384]{0:T(1024)S(1)}, s32[16384]{0:T(1024)}, u32[]{:S(2)}) copy-start(s32[16384]{0:T(1024)} %fusion.415) | copy-start | bytes 196612
  694.4 8.0 copy-start.19
  694.4 97.2 %all-to-all-start.1 = ((f32[8,2,2,16,16,128]{5,4,3,1,2,0:T(8,128)}), f32[8,2,2,16,16,128]{5,4,3,1,2,0:T(8,128)}, u32[]{:S(2)}, u32[]{:S(2)}) async-start(f32[8,2,2,16,16,128]{5,4,3,1,2,0:T(8,128)} %fusion.626), calls=%async_computation.1 | async-start | bytes 8388608 | tf_op jit(solution)/shard_map/while/body/eval_jaxpr/all_to_all | solution.py:12
  807.1 2.1 copy-start.5
  807.1 2.2 copy-start.6
  850.5 8.0 copy-start.19
  850.5 97.2 %all-to-all-start.1 = ((f32[8,2,2,16,16,128]{5,4,3,1,2,0:T(8,128)}), f32[8,2,2,16,16,128]{5,4,3,1,2,0:T(8,128)}, u32[]{:S(2)}, u32[]{:S(2)}) async-start(f32[8,2,2,16,16,128]{5,4,3,1,2,0:T(8,128)} %fusion.626), calls=%async_computation.1 | async-start | bytes 8388608 | tf_op jit(solution)/shard_map/while/body/eval_jaxpr/all_to_all | solution.py:12
  963.2 2.1 copy-start.5
  963.2 2.2 copy-start.6
  989.7 90.7 %copy-start.9 = (s32[16384]{0:T(1024)S(1)}, s32[16384]{0:T(1024)}, u32[]{:S(2)}) copy-start(s32[16384]{0:T(1024)} %param.16) | copy-start | bytes 196612
  989.7 90.6 %copy-start.10 = (f32[16384]{0:T(1024)S(1)}, f32[16384]{0:T(1024)}, u32[]{:S(2)}) copy-start(f32[16384]{0:T(1024)} %get-tuple-element.855) | copy-start | bytes 196612
  989.7 90.7 %copy-start.7 = (f32[3,16384]{1,0:T(4,128)S(1)}, f32[3,16384]{1,0:T(4,128)}, u32[]{:S(2)}) copy-start(f32[3,16384]{1,0:T(4,128)} %get-tuple-element.854) | copy-start | bytes 589828
  989.7 90.7 %copy-start.8 = (f32[3,16384]{1,0:T(4,128)S(1)}, f32[3,16384]{1,0:T(4,128)}, u32[]{:S(2)}) copy-start(f32[3,16384]{1,0:T(4,128)} %get-tuple-element.856) | copy-start | bytes 589828
  989.7 90.7 %copy-start.15 = (f32[3,3]{1,0:T(4,128)S(1)}, f32[3,3]{1,0:T(4,128)}, u32[]{:S(2)}) copy-start(f32[3,3]{1,0:T(4,128)} %fusion.418) | copy-start | bytes 112
  989.8 91.2 %copy-start.12 = (f32[16384]{0:T(1024)S(1)}, f32[16384]{0:T(1024)}, u32[]{:S(2)}) copy-start(f32[16384]{0:T(1024)} %get-tuple-element.1105) | copy-start | bytes 196612
  989.8 91.2 %copy-start.13 = (f32[16384]{0:T(1024)S(1)}, f32[16384]{0:T(1024)}, u32[]{:S(2)}) copy-start(f32[16384]{0:T(1024)} %get-tuple-element.1107) | copy-start | bytes 196612
  989.8 91.2 %copy-start.14 = (f32[16384]{0:T(1024)S(1)}, f32[16384]{0:T(1024)}, u32[]{:S(2)}) copy-start(f32[16384]{0:T(1024)} %get-tuple-element.1106) | copy-start | bytes 196612
  989.8 91.2 %copy-start.16 = (f32[16,32]{1,0:T(8,128)S(1)}, f32[16,32]{1,0:T(8,128)}, u32[]{:S(2)}) copy-start(f32[16,32]{1,0:T(8,128)} %custom-call.6) | copy-start | bytes 6148
  989.8 91.2 %copy-start.20 = (f32[4]{0:T(128)S(1)}, f32[4]{0:T(128)}, u32[]{:S(2)}) copy-start(f32[4]{0:T(128)} %mul.627) | copy-start | bytes 52
